TPU v7x, 8 devices: a whole 2x2x1 slice. The times are simulated.
8 devices in a mesh: rep: 1 (over z), tp: 2 (over y), sp: 4 (over x, core).
Axes of the slice: x: 2, y: 2, z: 1, core: 2. Of those that a mesh axis runs over, the one named last changes fastest.
Arguments:
- x_in: bfloat16 [2048, 4608], P(('rep', 'sp'))
- positions: int32 [2048], P(('rep', 'sp'))
- norm_gain: float32 [4608], replicated
- w_q: bfloat16 [4608, 4096], P(None, 'tp')
- w_k: bfloat16 [4608, 2048], P(None, 'tp')
- w_v: bfloat16 [4608, 2048], P(None, 'tp')
- w_o: bfloat16 [4096, 4608], P('tp')
- w_gate: bfloat16 [4608, 36864], P(None, 'tp')
- w_up: bfloat16 [4608, 36864], P(None, 'tp')
- w_down: bfloat16 [36864, 4608], P('tp')
Outputs:
- output 1: bfloat16 [2048, 4608], P(('rep', 'sp'))
- output 2: bfloat16 [2048, 16, 128], P('rep', ('tp', 'sp'))
- output 3: bfloat16 [2048, 16, 128], P('rep', ('tp', 'sp'))
All inputs are finite; a program needn't handle non-finite values.
Results may differ from a plain program's by a relative error of at most 0.00250291.
Values are sent between devices in bfloat16 or wider.
A program may use at most 2.25 GiB of HBM per device.

v0:
```python
import jax
import jax.numpy as jnp
from jax import lax
from jax.sharding import PartitionSpec as P

HEAD_DIM = 128
EPS = 1e-6
ROPE_BASE = 500000.0
SCORE_SCALE = HEAD_DIM ** -0.5


def rms_norm(x_in, norm_gain):
    x_f32 = x_in.astype(jnp.float32)
    inv_rms = lax.rsqrt(jnp.mean(x_f32 * x_f32, axis=-1, keepdims=True) + EPS)
    return (x_f32 * inv_rms * norm_gain).astype(jnp.bfloat16)


def rope_tables(positions):
    inv_freq = ROPE_BASE ** (-(jnp.arange(HEAD_DIM // 2, dtype=jnp.float32) * (2.0 / HEAD_DIM)))
    angles = positions.astype(jnp.float32)[:, None] * inv_freq[None, :]
    return jnp.cos(angles)[:, None, :], jnp.sin(angles)[:, None, :]


def rotate(vectors, cos_tab, sin_tab):
    half_dim = HEAD_DIM // 2
    lower_part = vectors[..., :half_dim]
    upper_part = vectors[..., half_dim:]
    return jnp.concatenate([lower_part * cos_tab - upper_part * sin_tab, upper_part * cos_tab + lower_part * sin_tab], axis=-1).astype(jnp.bfloat16)


def gated_mlp(normed, w_gate, w_up, w_down):
    gate_acc = jnp.dot(normed, w_gate, preferred_element_type=jnp.float32)
    up_acc = jnp.dot(normed, w_up, preferred_element_type=jnp.float32)
    hidden = (jax.nn.silu(gate_acc) * up_acc).astype(jnp.bfloat16)
    return jnp.dot(hidden, w_down, preferred_element_type=jnp.float32)


def causal_attention(q_rows, k_keys, v_keys, q_offset):
    tokens_q = q_rows.shape[0]
    heads_here = q_rows.shape[1]
    key_count = k_keys.shape[0]
    cache_here = k_keys.shape[1]
    group_size = heads_here // cache_here
    tile_rows = min(tokens_q, 128)
    key_idx = jnp.arange(key_count)

    def attend_tile(tile_id):
        q_tile = lax.dynamic_slice_in_dim(q_rows, tile_id * tile_rows, tile_rows, axis=0).reshape(tile_rows, cache_here, group_size, HEAD_DIM)
        scores = jnp.einsum("qcgd,kcd->cgqk", q_tile, k_keys, preferred_element_type=jnp.float32) * SCORE_SCALE
        query_idx = q_offset + tile_id * tile_rows + jnp.arange(tile_rows)
        scores = jnp.where(key_idx[None, :] <= query_idx[:, None], scores, -jnp.inf)
        weights = jnp.exp(scores - jnp.max(scores, axis=-1, keepdims=True))
        weight_total = jnp.sum(weights, axis=-1)
        weighted_sum = jnp.einsum("cgqk,kcd->qcgd", weights.astype(jnp.bfloat16), v_keys, preferred_element_type=jnp.float32)
        return (weighted_sum / jnp.transpose(weight_total, (2, 0, 1))[..., None]).astype(jnp.bfloat16)

    attn_tiles = lax.map(attend_tile, jnp.arange(tokens_q // tile_rows))
    return attn_tiles.reshape(tokens_q, heads_here, HEAD_DIM)


def solution(mesh):
    sp_size = mesh.shape["sp"]
    row_spec = P(("rep", "sp"), None)
    cache_spec = P("rep", ("tp", "sp"), None)

    def layer_block(x_in, positions, norm_gain, w_q, w_k, w_v, w_o, w_gate, w_up, w_down):
        tok_local = x_in.shape[0]
        heads_tp = w_q.shape[1] // HEAD_DIM
        kv_tp = w_k.shape[1] // HEAD_DIM
        heads_dev = heads_tp // sp_size
        cache_tp = max(kv_tp, sp_size)
        cache_dev = cache_tp // sp_size
        kv_repeat = cache_tp // kv_tp
        normed = rms_norm(x_in, norm_gain)
        cos_tab, sin_tab = rope_tables(positions)
        q_rot = rotate(jnp.dot(normed, w_q, preferred_element_type=jnp.float32).reshape(tok_local, heads_tp, HEAD_DIM), cos_tab, sin_tab)
        k_rot = rotate(jnp.dot(normed, w_k, preferred_element_type=jnp.float32).reshape(tok_local, kv_tp, HEAD_DIM), cos_tab, sin_tab)
        v_val = jnp.dot(normed, w_v, preferred_element_type=jnp.float32).astype(jnp.bfloat16).reshape(tok_local, kv_tp, HEAD_DIM)
        q_send = q_rot.reshape(tok_local, sp_size, heads_dev, HEAD_DIM)
        k_send = jnp.repeat(k_rot, kv_repeat, axis=1).reshape(tok_local, sp_size, cache_dev, HEAD_DIM)
        v_send = jnp.repeat(v_val, kv_repeat, axis=1).reshape(tok_local, sp_size, cache_dev, HEAD_DIM)
        send_buf = jnp.concatenate([q_send, k_send, v_send], axis=2)
        recv_buf = lax.all_to_all(send_buf, "sp", 1, 0, tiled=True)
        recv_buf = recv_buf.reshape(tok_local * sp_size, heads_dev + 2 * cache_dev, HEAD_DIM)
        q_all = recv_buf[:, :heads_dev]
        k_all = recv_buf[:, heads_dev:heads_dev + cache_dev]
        v_all = recv_buf[:, heads_dev + cache_dev:]
        attn_heads = causal_attention(q_all, k_all, v_all, 0)
        attn_tok = lax.all_to_all(attn_heads, "sp", 0, 1, tiled=True).reshape(tok_local, heads_tp * HEAD_DIM)
        attn_sum = lax.psum(jnp.dot(attn_tok, w_o, preferred_element_type=jnp.float32), "tp")
        mlp_sum = lax.psum(gated_mlp(normed, w_gate, w_up, w_down), "tp")
        y_out = (x_in.astype(jnp.float32) + attn_sum + mlp_sum).astype(jnp.bfloat16)
        return y_out, k_all, v_all

    return jax.shard_map(
        layer_block,
        mesh=mesh,
        in_specs=(row_spec, P(("rep", "sp")), P(None), P(None, "tp"), P(None, "tp"), P(None, "tp"), P("tp", None), P(None, "tp"), P(None, "tp"), P("tp", None)),
        out_specs=(row_spec, cache_spec, cache_spec),
        check_vma=False,
    )
```

profile of v0, /device:TPU:0, one launch (start us, length us, event | category | flops | bytes accessed | tf_op | source)
XLA Modules:
  0.0 931.8 jit_solution(14232986758019551199)
XLA Ops:
  7.2 3.5 fusion.30
  10.9 7.9 convolution_convert_fusion
  19.7 9.2 convolution_bitcast_fusion.1
  29.4 13.0 %convolution_bitcast_fusion = f32[64,8,16,128]{3,1,2,0:T(8,128)S(1)} fusion(bf16[4608,2048]{1,0:T(8,128)(2,1)} %param.15, bf16[512,4608]{1,0:T(8,128)(2,1)S(1)} %bitcast.110, f32[4608]{0:T(1024)S(1)} %copy-done.5, f32[512]{0:T(512)S(1)} %add_rsqrt_fusion), kind=kOutput, calls=%fused_computation.36 | convolution fusion | flops 9673113600 | bytes 27807744 | tf_op jit(solution)/shard_map/dot_general | solution.py:76
  47.0 8.4 pad_maximum_fusion
  55.4 2.7 copy.57
  58.1 4.9 all-to-all-start
  63.0 99.6 %fusion.38 = f32[512,18432]{1,0:T(8,128)} fusion(bf16[4608,18432]{1,0:T(8,128)(2,1)} %param.19, bf16[512,4608]{1,0:T(8,128)(2,1)} %param.12, f32[4608]{0:T(1024)S(1)} %copy-done.5, f32[512]{0:T(512)S(1)} %add_rsqrt_fusion), kind=kOutput, calls=%fused_computation.46 | convolution fusion | flops 86982524928 | bytes 212357120 | tf_op jit(solution)/shard_map/dot_general | solution.py:32
  162.6 100.0 %multiply_convert_fusion.clone.4 = bf16[512,18432]{1,0:T(8,128)(2,1)} fusion(f32[512,18432]{1,0:T(8,128)} %fusion.38, bf16[4608,18432]{1,0:T(8,128)(2,1)} %param.20, bf16[512,4608]{1,0:T(8,128)(2,1)} %param.12, f32[4608]{0:T(1024)S(1)} %copy-done.5, f32[512]{0:T(512)S(1)} %add_rsqrt_fusion), kind=kOutput, calls=%fused_computation.22.clone.clone.clone.1 | convolution fusion | flops 87039148032 | bytes 231231488 | tf_op jit(solution)/shard_map/dot_general | solution.py:33
  262.6 2.5 slice.32
  265.1 5.7 fusion.43
  272.9 89.7 %while.11 = (s32[]{:T(128)}, bf16[16,128,2,2,128]{4,1,0,3,2:T(8,128)(2,1)}, s32[16]{0:T(128)S(1)}, bf16[2048,4,128]{2,1,0:T(4,128)(2,1)S(1)}, bf16[2048,2,128]{2...) while((s32[]{:T(128)}, ...), condition=%wide.region_4.5_spmd.clone, body=%wide.region_1.4_spmd.clone.sunk | while | flops 548797568 | bytes 20720848 | solution.py:57
  276.6 2.0 fusion.74
  287.8 1.9 fusion.74
  299.0 1.9 fusion.74
  304.6 2.0 fusion.74
  310.2 2.0 fusion.74
  315.8 2.0 fusion.74
  321.4 2.0 fusion.74
  327.1 2.0 fusion.74
  332.7 2.0 fusion.74
  343.9 2.0 fusion.74
  349.5 2.0 fusion.74
  355.1 1.9 fusion.74
  360.7 1.9 fusion.74
  362.7 4.6 copy.50
  367.3 4.5 all-to-all-start.1
  371.8 99.8 %fusion.28 = f32[512,4608]{1,0:T(8,128)} fusion(bf16[18432,4608]{1,0:T(8,128)(2,1)} %param.21, bf16[512,18432]{1,0:T(8,128)(2,1)} %multiply_convert_fusion.clone.4), kind=kOutput, calls=%fused_computation.23 | convolution fusion | flops 86973087744 | bytes 198180864 | tf_op jit(solution)/shard_map/dot_general | solution.py:35
  473.6 2.3 copy.52
  475.9 16.9 %fusion.44 = f32[512,4608]{1,0:T(8,128)} fusion(bf16[512,2048]{0,1:T(8,128)(2,1)} %bitcast.118, bf16[2048,4608]{1,0:T(8,128)(2,1)} %param.18), kind=kOutput, calls=%fused_computation.48 | convolution fusion | flops 9663676416 | bytes 30408704 | tf_op jit(solution)/shard_map/dot_general | solution.py:90
  492.8 420.6 %all-reduce.3.cloned.1.call-done = (f32[512,4608]{1,0:T(8,128)}, f32[512,4608]{1,0:T(8,128)}) async-done(((f32[512,4608]{1,0:T(8,128)}, f32[512,4608]{1,0:T(8,128)}), (f32[512,4608]{1,0:T(8,128)}, f32[512,4608]{1,0:T(8,128)})) %all-reduce.3.cloned.1.call-update) | async-done | bytes 18874384 | tf_op jit(solution)/shard_map/psum | solution.py:91
  913.4 11.1 %fusion.34 = bf16[512,4608]{1,0:T(8,128)(2,1)} fusion(f32[512,4608]{1,0:T(8,128)} %get-tuple-element.91, f32[512,4608]{1,0:T(8,128)} %get-tuple-element.92, bf16[512,4608]{1,0:T(8,128)(2,1)} %param.12), kind=kLoop, calls=%fused_computation.32 | loop fusion | flops 9437184 | bytes 28311552 | tf_op jit(solution)/shard_map/convert_element_type | solution.py:92
  (180 shorter events, 63.2 us)
Async XLA Ops:
  7.2 3.8 copy-start
  10.9 8.7 copy-start.5
  18.8 10.6 %slice-start = ((s8[4718592]{0:T(1024)(128)(4,1)}), s8[524288]{0:T(1024)(128)(4,1)S(1)}, s32[]{:S(2)}) async-start(s8[4718592]{0:T(1024)(128)(4,1)} %bitcast.109), calls=%async_computation.3 | async-start | bytes 1048576
  19.6 9.7 %copy-start.4 = (s32[512]{0:T(512)S(1)}, s32[512]{0:T(512)}, u32[]{:S(2)}) copy-start(s32[512]{0:T(512)} %param.13) | copy-start | bytes 6148
  19.7 9.8 %slice-start.1 = ((s8[4718592]{0:T(1024)(128)(4,1)}), s8[4194304]{0:T(1024)(128)(4,1)S(1)}, s32[]{:S(2)}) async-start(s8[4718592]{0:T(1024)(128)(4,1)} %bitcast.109), calls=%async_computation.4 | async-start | bytes 8388608
  58.1 204.5 %all-to-all-start = ((bf16[512,4,8,128]{3,2,0,1:T(8,128)(2,1)}), bf16[512,4,8,128]{3,2,0,1:T(8,128)(2,1)}, u32[]{:S(2)}, u32[]{:S(2)}) async-start(bf16[512,4,8,128]{3,2,0,1:T(8,128)(2,1)} %copy.57), calls=%async_computation | async-start | bytes 8388608 | tf_op jit(solution)/shard_map/all_to_all | solution.py:83
  270.8 1.0 copy-start.1
  270.9 2.1 copy-start.2
  274.5 2.1 copy-start.3
  280.1 2.1 copy-start.3
  285.7 2.1 copy-start.3
  291.3 2.1 copy-start.3
  296.9 2.1 copy-start.3
  302.5 2.1 copy-start.3
  308.1 2.1 copy-start.3
  313.7 2.1 copy-start.3
  319.4 2.1 copy-start.3
  325.0 2.1 copy-start.3
  330.6 2.1 copy-start.3
  336.2 2.1 copy-start.3
  341.8 2.1 copy-start.3
  347.4 2.1 copy-start.3
  353.0 2.1 copy-start.3
  358.6 2.1 copy-start.3
  367.3 104.4 %all-to-all-start.1 = ((bf16[2048,4,128]{2,1,0:T(4,128)(2,1)}), bf16[2048,4,128]{2,1,0:T(4,128)(2,1)}, u32[]{:S(2)}, u32[]{:S(2)}) async-start(bf16[2048,4,128]{2,1,0:T(4,128)(2,1)} %copy.50), calls=%async_computation.1 | async-start | bytes 4194304 | tf_op jit(solution)/shard_map/all_to_all | solution.py:89
  371.8 541.6 %all-reduce.3.cloned.1.call-start = ((), (), s32[]{:S(2)}) async-start(), calls=%async_computation.2 | async-start | bytes 37748736 | tf_op jit(solution)/shard_map/psum | solution.py:91
Sparse Core Ops, SparseCore 0:
  492.9 420.4 all-reduce.2
where the time goes:
time: 947 us; the launch traced here: 932 us
  waiting for transfers between devices  421 us (44%)
  matrix products  393 us (41%)
  other arithmetic  47.9 us (5%)
  local copies, waits for them, and re-layouts  35.3 us (4%)
  between operations  14.6 us (2%)
  loops' own time  11.1 us (1%)
    psum x1, waiting for transfers between devices, layer_block(): mlp_sum = lax.psum(gated_mlp(normed, w_gate, w_up, w_down), 'tp')  421 us
    dot_general x1, matrix products, gated_mlp(): up_acc = jnp.dot(normed, w_up, preferred_element_type=jnp.float32)  100 us
    dot_general x1, matrix products, gated_mlp(): return jnp.dot(hidden, w_down, preferred_element_type=jnp.float32)  99.8 us
    dot_general x1, matrix products, gated_mlp(): gate_acc = jnp.dot(normed, w_gate, preferred_element_type=jnp.float32)  99.6 us
    dot_general x16, matrix products, attend_tile(): jnp.einsum('cgqk,kcd->qcgd', weights.astype(jnp.bfloat16), v_keys, prefer...  31.3 us
  transfers between devices with their start and end apart: 3, of which 1 were waited for; matrix products, arithmetic and copies ran while one was open for 32% of the time, Pallas kernels for 0%

commit v1 on v0

v1 whole, which is shorter than its diff:
```python
import functools
import math

import jax
import jax.numpy as jnp
from jax import lax
from jax.experimental import pallas as pl
from jax.experimental.pallas import tpu as pltpu
from jax.sharding import PartitionSpec as P

HEAD_DIM = 128
EPS = 1e-6
ROPE_BASE = 500000.0
EXP2_SCALE = HEAD_DIM ** -0.5 * math.log2(math.e)
VMEM_LIMIT = 63 * 2 ** 20
TILE = 512
SHARED_TILES = (11, 12)


def call_params(**kwargs):
    return pltpu.CompilerParams(vmem_limit_bytes=VMEM_LIMIT, **kwargs)


def rope_tables(positions):
    inv_freq = ROPE_BASE ** (-(jnp.arange(HEAD_DIM // 2, dtype=jnp.float32) * (2.0 / HEAD_DIM)))
    angles = positions.astype(jnp.float32)[:, None] * inv_freq[None, :]
    cos_half, sin_half = jnp.cos(angles), jnp.sin(angles)
    return jnp.concatenate([cos_half, cos_half], axis=-1), jnp.concatenate([-sin_half, sin_half], axis=-1)


def project_kernel(x_ref, gain_ref, cos_ref, sin_ref, w_q_ref, w_k_ref, w_v_ref, normed_ref, send_ref):
    @pl.when(pl.program_id(0) == 0)
    def _():
        rows = 64

        def norm_rows(step, carry):
            sl = pl.ds(pl.multiple_of(step * rows, rows), rows)
            x_f32 = x_ref[sl, :].astype(jnp.float32)
            inv_rms = lax.rsqrt(jnp.mean(x_f32 * x_f32, axis=-1, keepdims=True) + EPS)
            normed_ref[sl, :] = (x_f32 * inv_rms * gain_ref[...]).astype(jnp.bfloat16)
            return carry

        lax.fori_loop(0, x_ref.shape[0] // rows, norm_rows, 0)

    base = 0
    for w_ref, rotated in ((w_q_ref, True), (w_k_ref, True), (w_v_ref, False)):
        acc = jnp.dot(normed_ref[...], w_ref[...], preferred_element_type=jnp.float32)
        for lo in range(0, w_ref.shape[1], HEAD_DIM):
            head = acc[:, lo:lo + HEAD_DIM]
            if rotated:
                head = head * cos_ref[...] + pltpu.roll(head, HEAD_DIM // 2, 1) * sin_ref[...]
            send_ref[0, :, base + lo:base + lo + HEAD_DIM] = head.astype(jnp.bfloat16)
        base += w_ref.shape[1]


def project(x_in, norm_gain, cos_tab, sin_tab, w_q, w_k, w_v, sp_size):
    tokens, width = x_in.shape
    dq, dk = w_q.shape[1] // sp_size, w_k.shape[1] // sp_size
    whole = lambda shape: pl.BlockSpec(shape, lambda d: (0, 0))
    cols = lambda n: pl.BlockSpec((width, n), lambda d: (0, d))
    return pl.pallas_call(
        project_kernel,
        grid=(sp_size,),
        in_specs=[whole((tokens, width)), whole((1, width)), whole((tokens, HEAD_DIM)), whole((tokens, HEAD_DIM)), cols(dq), cols(dk), cols(dk)],
        out_specs=[whole((tokens, width)), pl.BlockSpec((1, tokens, dq + 2 * dk), lambda d: (d, 0, 0))],
        out_shape=[jax.ShapeDtypeStruct((tokens, width), jnp.bfloat16), jax.ShapeDtypeStruct((sp_size, tokens, dq + 2 * dk), jnp.bfloat16)],
        compiler_params=call_params(),
        cost_estimate=pl.CostEstimate(flops=2 * tokens * width * (dq + 2 * dk) * sp_size, bytes_accessed=2 * width * (dq + 2 * dk) * sp_size, transcendentals=0),
        name="project",
    )(x_in, norm_gain.reshape(1, width), cos_tab, sin_tab, w_q, w_k, w_v)


def gate_up_kernel(normed_ref, w_gate_ref, w_up_ref, hidden_ref):
    gate_acc = jnp.dot(normed_ref[...], w_gate_ref[...], preferred_element_type=jnp.float32)
    up_acc = jnp.dot(normed_ref[...], w_up_ref[...], preferred_element_type=jnp.float32)
    hidden_ref[...] = (jax.nn.silu(gate_acc) * up_acc).astype(jnp.bfloat16)


def gate_up(normed, w_gate, w_up, first, count, name):
    tokens, width = normed.shape
    w_spec = pl.BlockSpec((width, TILE), lambda i: (0, first + i))
    return pl.pallas_call(
        gate_up_kernel,
        grid=(count,),
        in_specs=[pl.BlockSpec((tokens, width), lambda i: (0, 0)), w_spec, w_spec],
        out_specs=pl.BlockSpec((tokens, TILE), lambda i: (0, i)),
        out_shape=jax.ShapeDtypeStruct((tokens, count * TILE), jnp.bfloat16),
        compiler_params=call_params(),
        cost_estimate=pl.CostEstimate(flops=4 * tokens * width * TILE * count, bytes_accessed=4 * width * TILE * count, transcendentals=tokens * TILE * count),
        name=name,
    )(normed, w_gate, w_up)


def attend_kernel(q_ref, k_ref, v_ref, out_ref, *, key_step):
    rows = q_ref.shape[0]
    group = q_ref.shape[1] // HEAD_DIM
    tile = pl.program_id(1)
    per_step = key_step // rows
    for step in range(k_ref.shape[0] // key_step):
        keys = (step + 1) * key_step

        @pl.when(tile // per_step == step)
        def _():
            row_idx = tile * rows + lax.broadcasted_iota(jnp.int32, (rows, key_step), 0)
            col_idx = step * key_step + lax.broadcasted_iota(jnp.int32, (rows, key_step), 1)
            for h in range(group):
                q_head = q_ref[:, h * HEAD_DIM:(h + 1) * HEAD_DIM]
                scores = []
                for j in range(step + 1):
                    s = lax.dot_general(q_head, k_ref[j * key_step:(j + 1) * key_step, :], (((1,), (1,)), ((), ())), preferred_element_type=jnp.float32)
                    if j == step:
                        s = jnp.where(col_idx <= row_idx, s, -jnp.inf)
                    scores.append(s)
                top = functools.reduce(jnp.maximum, [jnp.max(s, axis=-1, keepdims=True) for s in scores]) * EXP2_SCALE
                weights = [jnp.exp2(s * EXP2_SCALE - top) for s in scores]
                total = functools.reduce(jnp.add, [jnp.sum(w, axis=-1, keepdims=True) for w in weights])
                packed = jnp.concatenate([w.astype(jnp.bfloat16) for w in weights], axis=-1)
                mixed = jnp.dot(packed, v_ref[0:keys, :], preferred_element_type=jnp.float32)
                out_ref[:, h * HEAD_DIM:(h + 1) * HEAD_DIM] = (mixed / total).astype(jnp.bfloat16)


def attend(qkv, heads, caches):
    tokens = qkv.shape[0]
    rows, key_step = 256, 512
    group = heads // caches
    return pl.pallas_call(
        functools.partial(attend_kernel, key_step=key_step),
        grid=(caches, tokens // rows),
        in_specs=[
            pl.BlockSpec((rows, group * HEAD_DIM), lambda c, i: (i, c)),
            pl.BlockSpec((tokens, HEAD_DIM), lambda c, i: (0, heads + c)),
            pl.BlockSpec((tokens, HEAD_DIM), lambda c, i: (0, heads + caches + c)),
        ],
        out_specs=pl.BlockSpec((rows, group * HEAD_DIM), lambda c, i: (i, c)),
        out_shape=jax.ShapeDtypeStruct((tokens, heads * HEAD_DIM), jnp.bfloat16),
        compiler_params=call_params(),
        cost_estimate=pl.CostEstimate(flops=2 * 2 * tokens * tokens * HEAD_DIM * heads, bytes_accessed=4 * tokens * heads * HEAD_DIM, transcendentals=tokens * tokens * heads // 2),
        name="attend",
    )(qkv, qkv, qkv)


def finish_kernel(x_ref, normed_ref, attn_ref, hid_a_ref, hid_b_ref, w_gate_ref, w_up_ref, w_down_ref, w_o_ref, y_ref,
                  slots, wide, rows_u, part_out, part_in, y_buf,
                  slot_sem, load_sem, x_sem, part_send, part_recv, y_local, y_send, y_recv):
    me = lax.axis_index("tp")
    peer = {"tp": 1 - me}
    half = rows_u.shape[0]
    width = normed_ref.shape[1]
    ff = w_down_ref.shape[0]
    depth = slots.shape[1]
    lead = ff - depth
    tiles = y_buf.shape[0]
    split = hid_a_ref.shape[1]
    shared = split + hid_b_ref.shape[1]
    rest = (ff - shared) // TILE
    srcs, head_cols = attn_ref.shape[0], attn_ref.shape[2]

    def copy(src, dst, sem):
        return pltpu.make_async_copy(src, dst, sem)

    def down_copies(n, k, slot):
        cols = pl.ds(pl.multiple_of(n * TILE, TILE), TILE)
        if k == 0:
            return [copy(w_down_ref.at[pl.ds(0, depth), cols], slots.at[slot], slot_sem.at[slot, 0])]
        return [
            copy(w_down_ref.at[pl.ds(depth, lead), cols], slots.at[slot, pl.ds(0, lead)], slot_sem.at[slot, 0]),
            copy(w_o_ref.at[:, cols], slots.at[slot, pl.ds(lead, depth - lead)], slot_sem.at[slot, 1]),
        ]

    def rest_copies(r, slot):
        cols = pl.ds(pl.multiple_of(shared + r * TILE, TILE), TILE)
        return [
            copy(w_gate_ref.at[:, cols], slots.at[slot, pl.ds(0, width)], slot_sem.at[slot, 0]),
            copy(w_up_ref.at[:, cols], slots.at[slot, pl.ds(width, width)], slot_sem.at[slot, 1]),
        ]

    def start(copies):
        for c in copies:
            c.start()

    def wait(copies):
        for c in copies:
            c.wait()

    def row_loads(row):
        loads = [copy(hid_a_ref.at[pl.ds(row, half), :], wide.at[:, pl.ds(0, split)], load_sem.at[0]),
                 copy(hid_b_ref.at[pl.ds(row, half), :], wide.at[:, pl.ds(split, shared - split)], load_sem.at[1])]
        for s in range(srcs):
            loads.append(copy(attn_ref.at[s, pl.ds(row, half), :], wide.at[:, pl.ds(ff + s * head_cols, head_cols)], load_sem.at[2 + s]))
        return loads

    row_peer = pl.multiple_of((1 - me) * half, half)
    row_mine = pl.multiple_of(me * half, half)

    def part_copy(n):
        return pltpu.make_async_remote_copy(part_out.at[n], part_in.at[n], part_send.at[n], part_recv.at[n], device_id=peer, device_id_type=pl.DeviceIdType.MESH)

    def y_window(n):
        return y_ref.at[pl.ds(row_mine, half), pl.ds(pl.multiple_of(n * TILE, TILE), TILE)]

    def y_copy(n):
        return pltpu.make_async_remote_copy(y_buf.at[n], y_window(n), y_send.at[n], y_recv.at[n], device_id=peer, device_id_type=pl.DeviceIdType.MESH)

    def y_keep(n):
        return copy(y_buf.at[n], y_window(n), y_local.at[n])

    def x_load(n):
        return copy(x_ref.at[pl.ds(row_mine, half), pl.ds(n * TILE, TILE)], y_buf.at[n], x_sem.at[n])

    u_load = copy(normed_ref.at[pl.ds(row_peer, half), :], rows_u, load_sem.at[2 + srcs])
    u_load.start()
    start(rest_copies(0, 0))
    start(rest_copies(1, 1))
    loads = row_loads(row_peer)
    start(loads)
    for n in range(tiles):
        x_load(n).start()

    barrier = pltpu.get_barrier_semaphore()
    pl.semaphore_signal(barrier, inc=1, device_id=peer, device_id_type=pl.DeviceIdType.MESH)
    pl.semaphore_wait(barrier, 1)
    u_load.wait()

    def rest_phase(first):
        def rest_step(r, carry):
            slot = lax.rem(first + r, 3)
            ahead = lax.rem(first + r + 2, 3)
            wait(rest_copies(r, slot))

            @pl.when(r + 2 < rest)
            def _():
                start(rest_copies(r + 2, ahead))

            @pl.when(r + 2 == rest)
            def _():
                start(down_copies(0, 0, ahead))

            @pl.when(r + 2 == rest + 1)
            def _():
                start(down_copies(0, 1, ahead))

            gate_acc = jnp.dot(rows_u[...], slots[slot, 0:width, :], preferred_element_type=jnp.float32)
            up_acc = jnp.dot(rows_u[...], slots[slot, width:2 * width, :], preferred_element_type=jnp.float32)
            cols = pl.ds(pl.multiple_of(shared + r * TILE, TILE), TILE)
            wide[:, cols] = (jax.nn.silu(gate_acc) * up_acc).astype(jnp.bfloat16)
            return carry

        lax.fori_loop(0, rest, rest_step, 0)

    def down_phase(first, begin_tile, finish_tile, after):
        def tile_step(n, carry):
            begin_tile(n)
            for k in range(2):
                slot = lax.rem(first + 2 * n + k, 3)
                ahead = lax.rem(first + 2 * n + k + 2, 3)
                wait(down_copies(n, k, slot))

                @pl.when(n + 1 < tiles)
                def _():
                    start(down_copies(n + 1, k, ahead))

                if after is not None:
                    @pl.when(n + 1 == tiles)
                    def _():
                        start(after(k, ahead))

                if k == 0:
                    part_out[n] = jnp.dot(wide[:, 0:depth], slots[slot], preferred_element_type=jnp.float32)
                else:
                    finish_tile(n, jnp.dot(wide[:, depth:2 * depth], slots[slot], preferred_element_type=jnp.float32))
            return carry

        lax.fori_loop(0, tiles, tile_step, 0)

    rest_phase(0)
    wait(loads)

    def begin_peer(n):
        @pl.when(n > 0)
        def _():
            part_copy(n - 1).start()

    def finish_peer(n, dot):
        part_out[n] = part_out[n] + dot

    down_phase(rest, begin_peer, finish_peer, rest_copies)
    part_copy(tiles - 1).start()

    loads = row_loads(row_mine)
    start(loads)
    u_load = copy(normed_ref.at[pl.ds(row_mine, half), :], rows_u, load_sem.at[2 + srcs])
    u_load.start()
    for n in range(tiles):
        x_load(n).wait()
    u_load.wait()
    rest_phase(rest + 2 * tiles)
    wait(loads)

    def begin_mine(n):
        @pl.when(n > 0)
        def _():
            y_keep(n - 1).start()
            y_copy(n - 1).start()
        part_copy(n).wait_send()

    def finish_mine(n, dot):
        part_copy(n).wait_recv()
        total = y_buf[n].astype(jnp.float32) + (part_out[n] + dot + part_in[n])
        y_buf[n] = total.astype(jnp.bfloat16)

    down_phase(2 * rest + 2 * tiles, begin_mine, finish_mine, None)
    y_keep(tiles - 1).start()
    y_copy(tiles - 1).start()

    def drain(n, carry):
        y_keep(n).wait()
        y_copy(n).wait()
        return carry

    lax.fori_loop(0, tiles, drain, 0)


def finish(x_in, normed, attn, hid_a, hid_b, w_gate, w_up, w_down, w_o):
    tokens, width = x_in.shape
    half = tokens // 2
    ff = w_down.shape[0]
    deep = ff + w_o.shape[0]
    tiles = width // TILE
    anywhere = pl.BlockSpec(memory_space=pl.ANY)
    dma = pltpu.SemaphoreType.DMA
    return pl.pallas_call(
        finish_kernel,
        in_specs=[anywhere] * 9,
        out_specs=anywhere,
        out_shape=jax.ShapeDtypeStruct((tokens, width), jnp.bfloat16),
        scratch_shapes=[
            pltpu.VMEM((3, deep // 2, TILE), jnp.bfloat16),
            pltpu.VMEM((half, deep), jnp.bfloat16),
            pltpu.VMEM((half, width), jnp.bfloat16),
            pltpu.VMEM((tiles, half, TILE), jnp.float32),
            pltpu.VMEM((tiles, half, TILE), jnp.float32),
            pltpu.VMEM((tiles, half, TILE), jnp.bfloat16),
            dma((3, 2)),
            dma((3 + attn.shape[0],)),
            dma((tiles,)), dma((tiles,)), dma((tiles,)), dma((tiles,)), dma((tiles,)), dma((tiles,)),
        ],
        compiler_params=call_params(collective_id=0, has_side_effects=True),
        cost_estimate=pl.CostEstimate(flops=4 * tokens * width * ff, bytes_accessed=4 * width * ff, transcendentals=0),
        name="finish",
    )(x_in, normed, attn, hid_a, hid_b, w_gate, w_up, w_down, w_o)


def solution(mesh):
    sp_size = mesh.shape["sp"]
    row_spec = P(("rep", "sp"), None)
    cache_spec = P("rep", ("tp", "sp"), None)

    def layer_block(x_in, positions, norm_gain, w_q, w_k, w_v, w_o, w_gate, w_up, w_down):
        tok_local = x_in.shape[0]
        heads_dev = w_q.shape[1] // HEAD_DIM // sp_size
        cache_dev = w_k.shape[1] // HEAD_DIM // sp_size
        cos_tab, sin_tab = rope_tables(positions)
        normed, send_buf = project(x_in, norm_gain, cos_tab, sin_tab, w_q, w_k, w_v, sp_size)
        recv_buf = lax.all_to_all(send_buf, "sp", 0, 0, tiled=True)
        hid_a = gate_up(normed, w_gate, w_up, 0, SHARED_TILES[0], "gate_up_a")
        recv_buf, hid_a, normed_b = lax.optimization_barrier((recv_buf, hid_a, normed))
        qkv = recv_buf.reshape(tok_local * sp_size, -1)
        attn_heads = attend(qkv, heads_dev, cache_dev)
        attn_send = attn_heads.reshape(sp_size, tok_local, heads_dev * HEAD_DIM)
        attn_send, normed_c = lax.optimization_barrier((attn_send, normed_b))
        attn_recv = lax.all_to_all(attn_send, "sp", 0, 0, tiled=True)
        hid_b = gate_up(normed_c, w_gate, w_up, SHARED_TILES[0], SHARED_TILES[1], "gate_up_b")
        y_out = finish(x_in, normed_c, attn_recv, hid_a, hid_b, w_gate, w_up, w_down, w_o)
        k_all = qkv[:, heads_dev * HEAD_DIM:(heads_dev + cache_dev) * HEAD_DIM].reshape(-1, cache_dev, HEAD_DIM)
        v_all = qkv[:, (heads_dev + cache_dev) * HEAD_DIM:].reshape(-1, cache_dev, HEAD_DIM)
        return y_out, k_all, v_all

    return jax.shard_map(
        layer_block,
        mesh=mesh,
        in_specs=(row_spec, P(("rep", "sp")), P(None), P(None, "tp"), P(None, "tp"), P(None, "tp"), P("tp", None), P(None, "tp"), P(None, "tp"), P("tp", None)),
        out_specs=(row_spec, cache_spec, cache_spec),
        check_vma=False,
    )
```

time: 947 us -> 414 us (0.44); the launches traced: 932 us -> 414 us
  waiting for transfers between devices: 421 us -> 0.01 us
  matrix products: 393 us -> 0 us
  Pallas kernels: 0 us -> 391 us
  other arithmetic: 47.9 us -> 2.68 us
  local copies, waits for them, and re-layouts: 35.3 us -> 10.1 us
  between operations: 14.6 us -> 0.67 us
  loops' own time: 11.1 us -> 0 us
    psum x1 -> x0, waiting for transfers between devices: 421 us -> none  [layer_block(): mlp_sum = lax.psum(gated_mlp(normed, w_gate, w_up, w_down), 'tp')]
    dot_general x39 -> x0, matrix products: 393 us -> none  [the longest x1 100 us: gated_mlp(): up_acc = jnp.dot(normed, w_up, preferred_element_type=jnp.float32)]
    pallas_call x0 -> x5, Pallas kernels: none -> 391 us  [the longest x1 208 us: finish(): pl.pallas_call(finish_kernel, in_specs=[anywhere] * 9, out_specs=anywhere...]
    reduce_sum x17 -> x0, other arithmetic: 21.2 us -> none  [the longest x16 17.8 us: attend_tile(): weight_total = jnp.sum(weights, axis=-1)]
    convert_element_type x1 -> x0, other arithmetic: 11.1 us -> none  [layer_block(): y_out = (x_in.astype(jnp.float32) + attn_sum + mlp_sum).astype(jnp.bfloat16)]
    another operation x1 -> x0, loops' own time: 11.1 us -> none  [causal_attention(): attn_tiles = lax.map(attend_tile, jnp.arange(tokens_q // tile_rows))]
    dynamic_slice x48 -> x0, local copies, waits for them, and re-layouts: 10.9 us -> none  [the longest x16 9.71 us: causal_attention(): attn_tiles = lax.map(attend_tile, jnp.arange(tokens_q // tile_rows))]
  transfers between devices with their start and end apart: 3 -> 2, of which waited for: 1 -> 0; matrix products, arithmetic and copies ran while one was open for 32% -> 1% of each run, Pallas kernels for 0% -> 31%
where the time goes in v1:
time: 414 us
  Pallas kernels  391 us (94%)
  local copies, waits for them, and re-layouts  10.1 us (2%)
  starting transfers between devices  9.74 us (2%)
    pallas_call x1, Pallas kernels, finish(): pl.pallas_call(finish_kernel, in_specs=[anywhere] * 9, out_specs=anywhere...  208 us
    pallas_call x2, Pallas kernels, gate_up(): pl.pallas_call(gate_up_kernel, grid=(count,), in_specs=[pl.BlockSpec((tok...  128 us
    pallas_call x1, Pallas kernels, project(): pl.pallas_call(project_kernel, grid=(sp_size,), in_specs=[whole((tokens,...  30.1 us
    pallas_call x1, Pallas kernels, attend(): pl.pallas_call(functools.partial(attend_kernel, key_step=key_step), grid=...  24.3 us
  transfers between devices with their start and end apart: 2, of which 0 were waited for; matrix products, arithmetic and copies ran while one was open for 1% of the time, Pallas kernels for 31%

profile of v1, /device:TPU:0, one launch (start us, length us, event | category | flops | bytes accessed | tf_op | source)
XLA Modules:
  0.0 413.9 jit_solution(15039841675926283392)
XLA Ops:
  0.6 0.7 convert_element_type.3
  1.3 1.3 reshape.28.gain_ref
  2.7 1.0 fusion
  3.7 1.0 pad_maximum_fusion
  4.7 30.1 %project.1 = (bf16[512,4608]{1,0:T(8,128)(2,1)}, bf16[4,512,1024]{2,1,0:T(8,128)(2,1)}) custom-call(bf16[512,4608]{1,0:T(8,128)(2,1)} %x_ref.3, f32[1,4608]{1,0:T(1,128)} %reshape.28.gain_ref, f32[512,128]{1,0:T(8,128)} %get-tuple-element.22.cos_ref, f32[512,128]{1,0:T(8,128)} %get-tuple-element.23.sin_ref, bf16[4608,2048]{1,0:T(8,128)(2,1)} %w_q_ref.1, ...), custom_call_target="tpu_custom_call" | custom-call | flops 19327352832 | bytes 37748736 | tf_op jit(solution)/shard_map/project/pallas_call | solution.py:61
  34.7 5.1 %all-to-all-start = ((bf16[4,512,1024]{2,1,0:T(8,128)(2,1)}), bf16[4,512,1024]{2,1,0:T(8,128)(2,1)}, u32[]{:S(2)}, u32[]{:S(2)}) async-start(bf16[4,512,1024]{2,1,0:T(8,128)(2,1)} %get-tuple-element.10), calls=%async_computation | async-start | bytes 8388608 | tf_op jit(solution)/shard_map/all_to_all | solution.py:364
  39.8 61.7 %gate_up_a.1.hid_a_ref = bf16[512,5632]{1,0:T(8,128)(2,1)} custom-call(bf16[512,4608]{1,0:T(8,128)(2,1)} %get-tuple-element.14.normed_ref, bf16[4608,18432]{1,0:T(8,128)(2,1)} %w_gate_ref.5, bf16[4608,18432]{1,0:T(8,128)(2,1)} %w_up_ref.5), custom_call_target="tpu_custom_call" | custom-call | flops 53150220288 | bytes 103809024 | tf_op jit(solution)/shard_map/gate_up_a/pallas_call | solution.py:82
  101.5 0.0 all-to-all-done
  101.5 24.3 %attend.1 = bf16[2048,512]{1,0:T(8,128)(2,1)} custom-call(bf16[2048,1024]{1,0:T(8,128)(2,1)} %bitcast.q_ref.k_ref.v_ref, bf16[2048,1024]{1,0:T(8,128)(2,1)} %bitcast.q_ref.k_ref.v_ref, bf16[2048,1024]{1,0:T(8,128)(2,1)} %bitcast.q_ref.k_ref.v_ref), custom_call_target="tpu_custom_call" | custom-call | flops 8589934592 | bytes 4194304 | tf_op jit(solution)/shard_map/attend/pallas_call | solution.py:126
  125.8 4.7 %all-to-all-start.1 = ((bf16[4,512,512]{2,1,0:T(8,128)(2,1)}), bf16[4,512,512]{2,1,0:T(8,128)(2,1)}, u32[]{:S(2)}, u32[]{:S(2)}) async-start(bf16[4,512,512]{2,1,0:T(8,128)(2,1)} %bitcast.2), calls=%async_computation.1 | async-start | bytes 4194304 | tf_op jit(solution)/shard_map/all_to_all | solution.py:371
  130.5 66.8 %gate_up_b.1.hid_b_ref = bf16[512,6144]{1,0:T(8,128)(2,1)} custom-call(bf16[512,4608]{1,0:T(8,128)(2,1)} %get-tuple-element.14.normed_ref, bf16[4608,18432]{1,0:T(8,128)(2,1)} %w_gate_ref.5, bf16[4608,18432]{1,0:T(8,128)(2,1)} %w_up_ref.5), custom_call_target="tpu_custom_call" | custom-call | flops 57982058496 | bytes 113246208 | tf_op jit(solution)/shard_map/gate_up_b/pallas_call | solution.py:82
  197.3 1.7 fusion.1
  199.0 1.1 reshape.32
  200.1 1.1 reshape.31
  201.2 0.0 all-to-all-done.1.attn_ref
  201.2 207.9 %finish.1 = bf16[512,4608]{1,0:T(8,128)(2,1)} custom-call(bf16[512,4608]{1,0:T(8,128)(2,1)} %x_ref.3, bf16[512,4608]{1,0:T(8,128)(2,1)} %get-tuple-element.14.normed_ref, bf16[4,512,512]{2,1,0:T(8,128)(2,1)} %all-to-all-done.1.attn_ref, bf16[512,5632]{1,0:T(8,128)(2,1)} %gate_up_a.1.hid_a_ref, bf16[512,6144]{1,0:T(8,128)(2,1)} %gate_up_b.1.hid_b_ref, ...), custom_call_target="tpu_custom_call" | custom-call | flops 173946175488 | bytes 339738624 | tf_op jit(solution)/shard_map/finish/pallas_call | solution.py:331
  409.0 4.8 %copy.14 = bf16[512,4608]{1,0:T(8,128)(2,1)} copy(bf16[512,4608]{1,0:T(8,128)(2,1)} %finish.1) | data formatting | bytes 9437184
  (1 shorter events, 0.0 us)
Async XLA Ops:
  34.7 66.8 %all-to-all-start = ((bf16[4,512,1024]{2,1,0:T(8,128)(2,1)}), bf16[4,512,1024]{2,1,0:T(8,128)(2,1)}, u32[]{:S(2)}, u32[]{:S(2)}) async-start(bf16[4,512,1024]{2,1,0:T(8,128)(2,1)} %get-tuple-element.10), calls=%async_computation | async-start | bytes 8388608 | tf_op jit(solution)/shard_map/all_to_all | solution.py:364
  125.8 75.3 %all-to-all-start.1 = ((bf16[4,512,512]{2,1,0:T(8,128)(2,1)}), bf16[4,512,512]{2,1,0:T(8,128)(2,1)}, u32[]{:S(2)}, u32[]{:S(2)}) async-start(bf16[4,512,512]{2,1,0:T(8,128)(2,1)} %bitcast.2), calls=%async_computation.1 | async-start | bytes 4194304 | tf_op jit(solution)/shard_map/all_to_all | solution.py:371
